TPU v7x, 32 devices: a whole 2x2x4 slice. The times are simulated.
32 devices in a mesh: zero: 8 (over z, x), tp: 4 (over y, core).
Axes of the slice: x: 2, y: 2, z: 4, core: 2. Of those that a mesh axis runs over, the one named last changes fastest.
Arguments:
- train_gate: float32 [2048, 8192], P('zero', 'tp'), may hold values from -0.1875 to 0.1875
- slow_gate: float32 [2048, 8192], P('zero', 'tp'), may hold values from -0.125 to 0.125
- train_up: float32 [2048, 8192], P('zero', 'tp'), may hold values from -0.1875 to 0.1875
- slow_up: float32 [2048, 8192], P('zero', 'tp'), may hold values from -0.125 to 0.125
- norm_gain: float32 [2048], P('zero'), may hold values from 0.25 to 1.75
Outputs:
- serving_gate: bfloat16 [2048, 8192], P(None, 'tp')
- serving_up: bfloat16 [2048, 8192], P(None, 'tp')
- scale_gate: float32 [8192], P('tp')
- scale_up: float32 [8192], P('tp')
All inputs are finite; a program needn't handle non-finite values.
Results may differ from a plain program's by a relative error of at most 0.0004.
Values may be sent and summed in bfloat16 or wider, within the bound.
A program may use at most 128 MiB of HBM per device.

v0:
```python
import functools

import jax
import jax.numpy as jnp
from jax import lax
from jax.experimental import pallas as pl
from jax.experimental.pallas import tpu as pltpu
from jax.sharding import PartitionSpec as P

keep_rate = 0.75
MESH = pl.DeviceIdType.MESH
SIDE = 2
LANES = 128
GROUP = 8
HEAD = 16
LEAD = 16
VMEM_BYTES = 67_043_328


def gather_kernel(
    count, pieces, head,
    train_gate, slow_gate, train_up, slow_up, gain_ref,
    gate_ref, up_ref, scale_gate_ref, scale_up_ref,
    train, slow, gains, sums, heads,
    head_send, head_recv, load_sem, sum_send, sum_recv,
    left_send, left_recv, right_send, right_recv, side_send, side_recv, half_send, half_recv,
):
    length = count // SIDE
    rows, columns = train_gate.shape
    piece_rows = rows // pieces
    me = lax.axis_index("zero")
    place, side = me // SIDE, me % SIDE
    outs = (gate_ref, up_ref)
    scales = (scale_gate_ref, scale_up_ref)

    barrier = pltpu.get_barrier_semaphore()
    for step in range(1, count):
        pl.semaphore_signal(barrier, 1, device_id={"zero": lax.rem(me + step, count)}, device_id_type=MESH)

    loads = []
    for which, (t, s) in enumerate(((train_gate, slow_gate), (train_up, slow_up))):
        for p in range(pieces):
            at = pl.ds(p * piece_rows, piece_rows)
            k = (which * pieces + p) * 2
            loads.append((
                pltpu.make_async_copy(t.at[at], train.at[which, at], load_sem.at[k]),
                pltpu.make_async_copy(s.at[at], slow.at[which, at], load_sem.at[k + 1]),
            ))
    for pair in loads:
        for load in pair:
            load.start()

    gains[...] = jnp.broadcast_to(gain_ref[...], (LANES, rows)).T

    def sum_copy(which, step, source, to):
        k = which * (count - 1) + step - 1
        return pltpu.make_async_remote_copy(
            src_ref=sums.at[which, source], dst_ref=sums.at[which, source],
            send_sem=sum_send.at[k], recv_sem=sum_recv.at[k],
            device_id={"zero": to}, device_id_type=MESH,
        )

    to_left = jnp.maximum(place - 1, 0) * SIDE + side
    to_right = jnp.minimum(place + 1, length - 1) * SIDE + side
    to_side = place * SIDE + (SIDE - 1 - side)
    has_left, has_right = place > 0, place < length - 1
    for which in range(2):
        def add(i, total):
            at = pl.ds(pl.multiple_of(i * GROUP, GROUP), GROUP)
            gain = jnp.concatenate([gains[at, :]] * (columns // LANES), axis=1)
            gained = (keep_rate * slow[which, at, :] + (1.0 - keep_rate) * train[which, at, :]) * gain
            slow[which, at, :] = gained
            return total + gained * gained

        total = jnp.zeros((GROUP, columns), jnp.float32)
        for p in range(pieces):
            for load in loads[which * pieces + p]:
                load.wait()
            total = lax.fori_loop(p * piece_rows // GROUP, (p + 1) * piece_rows // GROUP, add, total)
        sums[which, me] = jnp.sum(total, axis=0, keepdims=True)
        if which == 0:
            pl.semaphore_wait(barrier, count - 1)
        for step in range(1, count):
            sum_copy(which, step, me, lax.rem(me + step, count)).start()

    def head_copy(slot, to):
        return pltpu.make_async_remote_copy(
            src_ref=slow.at[0, pl.ds(0, head)], dst_ref=heads.at[slot],
            send_sem=head_send.at[slot], recv_sem=head_recv.at[slot],
            device_id={"zero": to}, device_id_type=MESH,
        )

    @pl.when(has_left)
    def _():
        head_copy(0, to_left).start()

    @pl.when(has_right)
    def _():
        head_copy(1, to_right).start()

    head_copy(2, to_side).start()

    def part_of(owner_place, owner_side, which, p, skip=0):
        start = (owner_place * SIDE + owner_side) * rows + p * piece_rows + skip
        step = GROUP * 2 if skip else piece_rows
        return outs[which].at[pl.ds(pl.multiple_of(start, step), piece_rows - skip)]

    def skipped(distance, which, p):
        return head if (distance, which, p) == (0, 0, 0) else 0

    def copy_to(ref, send, recv, to):
        return pltpu.make_async_remote_copy(
            src_ref=ref, dst_ref=ref, send_sem=send, recv_sem=recv,
            device_id={"zero": to}, device_id_type=MESH,
        )

    is_even = place % 2 == 0
    twin = place + 1 - 2 * (place % 2)
    to_twin = twin * SIDE + side
    half_round = jnp.maximum(jnp.where(is_even, place, length - 1 - place), 1)
    order = [(which, p) for which in range(2) for p in range(pieces)]

    def left_copy(distance, which, p):
        k = distance * 2 * pieces + which * pieces + p
        return copy_to(part_of(place + distance, side, which, p, skipped(distance, which, p)), left_send.at[k], left_recv.at[k], to_left)

    def right_copy(distance, which, p):
        k = distance * 2 * pieces + which * pieces + p
        return copy_to(part_of(place - distance, side, which, p, skipped(distance, which, p)), right_send.at[k], right_recv.at[k], to_right)

    def side_index(distance, which, p):
        d = distance if distance >= 0 else length - 1 - distance
        return d * 2 * pieces + which * pieces + p

    def side_copy(distance, which, p):
        k = side_index(distance, which, p)
        return copy_to(part_of(place + distance, side, which, p, skipped(distance, which, p)), side_send.at[k], side_recv.at[k], to_side)

    def side_arrival(distance, which, p):
        k = side_index(distance, which, p)
        return copy_to(part_of(place + distance, SIDE - 1 - side, which, p, skipped(distance, which, p)), side_send.at[k], side_recv.at[k], to_side)

    def half_copy(p):
        return copy_to(part_of(place, SIDE - 1 - side, 1, p), half_send.at[p], half_recv.at[p], to_twin)

    def half_arrival(p):
        return copy_to(part_of(twin, SIDE - 1 - side, 1, p), half_send.at[p], half_recv.at[p], to_twin)

    def in_line(distance):
        return place + distance <= length - 1 if distance > 0 else place + distance >= 0

    def by_side(distance, which):
        ok = in_line(distance)
        if which == 1 and distance == 1:
            ok = jnp.logical_and(ok, jnp.logical_not(is_even))
        if which == 1 and distance == -1:
            ok = jnp.logical_and(ok, is_even)
        return ok

    def send_own(which, p):
        @pl.when(has_left)
        def _():
            left_copy(0, which, p).start()

        @pl.when(has_right)
        def _():
            right_copy(0, which, p).start()

        side_copy(0, which, p).start()

    for which in range(2):
        for step in range(1, count):
            source = lax.rem(me + count - step, count)
            sum_copy(which, step, source, source).wait_recv()
        total = sums[which, 0]
        for k in range(1, count):
            total = total + sums[which, k]
        scale = jnp.sqrt(total)
        scales[which][...] = scale
        inverse = 1.0 / scale
        def store(p, first, size):
            start = pl.multiple_of(me * rows + p * piece_rows + first, GROUP * 2)
            block = slow[which, pl.ds(p * piece_rows + first, size), :]
            outs[which][pl.ds(start, size), :] = (block * inverse).astype(jnp.bfloat16)

        for p in range(pieces + 1):
            if p < pieces:
                store(p, 0, LEAD)
            if p > 0:
                send_own(which, p - 1)
            if p < pieces:
                store(p, LEAD, piece_rows - LEAD)

        if which == 0:
            def use_head(slot, owner, sender):
                head_copy(slot, sender).wait_recv()
                start = pl.multiple_of(owner * rows, GROUP * 2)
                outs[0][pl.ds(start, head), :] = (heads[slot] * inverse).astype(jnp.bfloat16)

            @pl.when(has_right)
            def _():
                use_head(0, to_right, to_right)

            @pl.when(has_left)
            def _():
                use_head(1, to_left, to_left)

            use_head(2, to_side, to_side)

    for k in range(1, length):
        for which, p in order:
            @pl.when(in_line(k))
            def _():
                q = (k - 1) * 2 * pieces + which * pieces + p
                copy_to(part_of(place + k, side, which, p, skipped(k - 1, which, p)), left_send.at[q], left_recv.at[q], to_right).wait_recv()

                @pl.when(has_left)
                def _():
                    left_copy(k, which, p).start()

            @pl.when(by_side(k, which))
            def _():
                side_copy(k, which, p).start()

            @pl.when(in_line(-k))
            def _():
                q = (k - 1) * 2 * pieces + which * pieces + p
                copy_to(part_of(place - k, side, which, p, skipped(k - 1, which, p)), right_send.at[q], right_recv.at[q], to_left).wait_recv()

                @pl.when(has_right)
                def _():
                    right_copy(k, which, p).start()

            @pl.when(by_side(-k, which))
            def _():
                side_copy(-k, which, p).start()

        @pl.when(half_round == k)
        def _():
            for p in range(pieces):
                side_arrival(0, 1, p).wait_recv()
                half_copy(p).start()

    for p in range(pieces):
        side_arrival(0, 0, p).wait_recv()

    for k in range(1, length):
        for which, p in order:
            for distance in (k, -k):
                @pl.when(by_side(distance, which))
                def _():
                    side_arrival(distance, which, p).wait_recv()
                    side_copy(distance, which, p).wait_send()

    for p in range(pieces):
        half_arrival(p).wait_recv()
        half_copy(p).wait_send()

    for which in range(2):
        for step in range(1, count):
            sum_copy(which, step, me, lax.rem(me + step, count)).wait_send()

    @pl.when(has_left)
    def _():
        head_copy(0, to_left).wait_send()

    @pl.when(has_right)
    def _():
        head_copy(1, to_right).wait_send()

    head_copy(2, to_side).wait_send()
    for which, p in order:
        side_copy(0, which, p).wait_send()
        for k in range(length):
            @pl.when(jnp.logical_and(has_left, place + k <= length - 1))
            def _():
                left_copy(k, which, p).wait_send()

            @pl.when(jnp.logical_and(has_right, place - k >= 0))
            def _():
                right_copy(k, which, p).wait_send()


def store_kernel(parts, gate, up, scale_gate, scale_up, gate_out, up_out, scale_gate_out, scale_up_out, sem):
    rows = gate.shape[0] // parts
    copies = []
    for which, (held, out) in enumerate(((gate, gate_out), (up, up_out))):
        for k in range(parts):
            at = pl.ds(k * rows, rows)
            copies.append(pltpu.make_async_copy(held.at[at], out.at[at], sem.at[which * parts + k]))
    copies.append(pltpu.make_async_copy(scale_gate.at[0], scale_gate_out, sem.at[2 * parts]))
    copies.append(pltpu.make_async_copy(scale_up.at[0], scale_up_out, sem.at[2 * parts + 1]))
    for copy in copies:
        copy.start()
    for copy in copies:
        copy.wait()


def solution(mesh):
    count = mesh.shape["zero"]

    def body(train_gate, slow_gate, train_up, slow_up, norm_gain):
        rows, columns = train_gate.shape
        pieces = max(1, min(2, rows // 64))
        head = HEAD
        length = count // SIDE
        full = (rows * count, columns)
        block = pltpu.VMEM(full, jnp.bfloat16)
        scale = pltpu.VMEM((1, columns), jnp.float32)
        vmem, held = pl.BlockSpec(memory_space=pltpu.VMEM), pl.BlockSpec(memory_space=pltpu.HBM)
        dma = lambda n: pltpu.SemaphoreType.DMA((n,))
        line, wide = length * 2 * pieces, (2 * length - 1) * 2 * pieces
        gathered = pl.pallas_call(
            functools.partial(gather_kernel, count, pieces, head),
            out_shape=(block, block, scale, scale),
            in_specs=[held] * 4 + [vmem],
            out_specs=(vmem,) * 4,
            scratch_shapes=[
                pltpu.VMEM((2, rows, columns), jnp.float32),
                pltpu.VMEM((2, rows, columns), jnp.float32),
                pltpu.VMEM((rows, LANES), jnp.float32),
                pltpu.VMEM((2, count, 1, columns), jnp.float32),
                pltpu.VMEM((3, head, columns), jnp.float32),
                dma(3), dma(3), dma(4 * pieces), dma(2 * count - 2), dma(2 * count - 2),
                dma(line), dma(line), dma(line), dma(line), dma(wide), dma(wide), dma(pieces), dma(pieces),
            ],
            compiler_params=pltpu.CompilerParams(
                collective_id=0, has_side_effects=True,
                vmem_limit_bytes=VMEM_BYTES - 2 * full[0] * full[1] * 2 - (1 << 19),
            ),
        )(train_gate, slow_gate, train_up, slow_up, norm_gain[None, :])
        parts = 4
        return pl.pallas_call(
            functools.partial(store_kernel, parts),
            out_shape=(jax.ShapeDtypeStruct(full, jnp.bfloat16),) * 2 + (jax.ShapeDtypeStruct((columns,), jnp.float32),) * 2,
            in_specs=[vmem] * 4,
            out_specs=(held,) * 4,
            scratch_shapes=[dma(2 * parts + 2)],
            compiler_params=pltpu.CompilerParams(vmem_limit_bytes=1 << 20),
        )(*gathered)

    in_specs = (P("zero", "tp"), P("zero", "tp"), P("zero", "tp"), P("zero", "tp"), P("zero"))
    out_specs = (P(None, "tp"), P(None, "tp"), P("tp"), P("tp"))
    return jax.shard_map(body, mesh=mesh, in_specs=in_specs, out_specs=out_specs, check_vma=False)
```

profile of v0, /device:TPU:1, one launch (start us, length us, event | category | flops | bytes accessed | tf_op | source)
XLA Modules:
  0.0 176.0 jit_solution(1085924513938437617)
XLA Ops:
  0.6 169.4 %shard_map.84 = (bf16[2048,2048]{1,0:T(8,128)(2,1)S(1)}, bf16[2048,2048]{1,0:T(8,128)(2,1)S(1)}, f32[1,2048]{1,0:T(1,128)S(1)}, f32[1,2048]{1,0:T(1,128)S(1)}) custom-call(f32[256,2048]{1,0:T(8,128)} %train_gate.1, f32[256,2048]{1,0:T(8,128)} %slow_gate.1, f32[256,2048]{1,0:T(8,128)} %train_up.1, f32[256,2048]{1,0:T(8,128)} %slow_up.1, f32[1,256]{1,0:T(1,128)} %bitcast.1), custom_call_target="tpu_custom_call" | custom-call | tf_op jit(solution)/shard_map/pallas_call | solution.py:313
  170.1 5.9 %shard_map.85 = (bf16[2048,2048]{1,0:T(8,128)(2,1)}, bf16[2048,2048]{1,0:T(8,128)(2,1)}, f32[2048]{0:T(1024)}, f32[2048]{0:T(1024)}) custom-call(bf16[2048,2048]{1,0:T(8,128)(2,1)S(1)} %get-tuple-element.8.gate, bf16[2048,2048]{1,0:T(8,128)(2,1)S(1)} %get-tuple-element.9.up, f32[1,2048]{1,0:T(1,128)S(1)} %get-tuple-element.10.scale_gate, ...), custom_call_target="tpu_custom_call" | custom-call | tf_op jit(solution)/shard_map/pallas_call | solution.py:333
where the time goes:
time: 177 us; the launch traced here: 176 us
  Pallas kernels  175 us (99%)
    pallas_call x1, Pallas kernels, body(): pl.pallas_call(functools.partial(gather_kernel, count, pieces, head), out...  169 us
    pallas_call x1, Pallas kernels, body(): pl.pallas_call(functools.partial(store_kernel, parts), out_shape=(jax.Sha...  5.95 us

commit v1 on v0

v1 whole, which is shorter than its diff:
```python
import functools

import jax
import jax.numpy as jnp
from jax import lax
from jax.experimental import pallas as pl
from jax.experimental.pallas import tpu as pltpu
from jax.sharding import PartitionSpec as P

keep_rate = 0.75
MESH = pl.DeviceIdType.MESH
SIDE = 2
LANES = 128
GROUP = 8
HEAD = 16
LEAD = 16
SHARES = 16
GATE_RUNS = ((8, 0, False), (16, 0, True))
UP_RUNS = ((3, 0, False), (6, 0, True), (12, 1, False), (16, 2, True))
VMEM_BYTES = 67_043_328


def both(*conditions):
    kept = [c for c in conditions if c is not None]
    return functools.reduce(jnp.logical_and, kept) if kept else None


def when(condition):
    return (lambda f: f()) if condition is None else pl.when(condition)


class Relay:
    def __init__(self, count, rows, head, units, sources, outs, sems):
        self.rows, self.head, self.units, self.sources, self.outs = rows, head, units, sources, outs
        self.left_send, self.left_recv, self.right_send, self.right_recv, self.side_send, self.side_recv, self.half_send, self.half_recv = sems
        me = lax.axis_index("zero")
        self.length = count // SIDE
        self.place, self.side = me // SIDE, me % SIDE
        place, side, length = self.place, self.side, self.length
        self.to_left = jnp.maximum(place - 1, 0) * SIDE + side
        self.to_right = jnp.minimum(place + 1, length - 1) * SIDE + side
        self.to_side = place * SIDE + (SIDE - 1 - side)
        self.has_left, self.has_right = place > 0, place < length - 1
        self.is_even = place % 2 == 0
        self.twin = place + 1 - 2 * (place % 2)
        self.to_twin = self.twin * SIDE + side
        self.half_round = jnp.maximum(jnp.where(self.is_even, place, length - 1 - place), 1)

    def skipped(self, distance, u):
        return self.head if (distance, *self.units[u][:2]) == (0, 0, 0) else 0

    def copy(self, place, side, distance, u, send, recv, to, skip):
        which, first, size = self.units[u][:3]
        start = (place * SIDE + side) * self.rows + first + skip
        at = pl.ds(pl.multiple_of(start, GROUP * 2), size - skip)
        source = self.sources[which] if distance == 0 else self.outs[which]
        return pltpu.make_async_remote_copy(
            src_ref=source.at[at], dst_ref=self.outs[which].at[at], send_sem=send, recv_sem=recv,
            device_id={"zero": to}, device_id_type=MESH,
        )

    def index(self, distance, u):
        return distance * len(self.units) + u

    def left_copy(self, distance, u):
        k = self.index(distance, u)
        return self.copy(self.place + distance, self.side, distance, u, self.left_send.at[k], self.left_recv.at[k], self.to_left, self.skipped(distance, u))

    def left_arrival(self, distance, u):
        k = self.index(distance - 1, u)
        return self.copy(self.place + distance, self.side, 1, u, self.left_send.at[k], self.left_recv.at[k], self.to_right, self.skipped(distance - 1, u))

    def right_copy(self, distance, u):
        k = self.index(distance, u)
        return self.copy(self.place - distance, self.side, distance, u, self.right_send.at[k], self.right_recv.at[k], self.to_right, self.skipped(distance, u))

    def right_arrival(self, distance, u):
        k = self.index(distance - 1, u)
        return self.copy(self.place - distance, self.side, 1, u, self.right_send.at[k], self.right_recv.at[k], self.to_left, self.skipped(distance - 1, u))

    def side_index(self, distance, u):
        return self.index(distance if distance >= 0 else self.length - 1 - distance, u)

    def side_copy(self, distance, u):
        k = self.side_index(distance, u)
        return self.copy(self.place + distance, self.side, distance, u, self.side_send.at[k], self.side_recv.at[k], self.to_side, self.skipped(distance, u))

    def side_arrival(self, distance, u):
        k = self.side_index(distance, u)
        return self.copy(self.place + distance, SIDE - 1 - self.side, 1, u, self.side_send.at[k], self.side_recv.at[k], self.to_side, self.skipped(distance, u))

    def half_copy(self, u):
        return self.copy(self.place, SIDE - 1 - self.side, 1, u, self.half_send.at[u], self.half_recv.at[u], self.to_twin, 0)

    def half_arrival(self, u):
        return self.copy(self.twin, SIDE - 1 - self.side, 1, u, self.half_send.at[u], self.half_recv.at[u], self.to_twin, 0)

    def is_half(self, u):
        return self.units[u][4]

    def in_line(self, distance):
        return self.place + distance <= self.length - 1 if distance > 0 else self.place + distance >= 0

    def by_side(self, distance, u):
        ok = self.in_line(distance)
        if self.is_half(u) and distance == 1:
            ok = jnp.logical_and(ok, jnp.logical_not(self.is_even))
        if self.is_half(u) and distance == -1:
            ok = jnp.logical_and(ok, self.is_even)
        return ok

    def send_own(self, u):
        condition = self.units[u][3]

        @when(both(condition, self.has_left))
        def _():
            self.left_copy(0, u).start()

        @when(both(condition, self.has_right))
        def _():
            self.right_copy(0, u).start()

        @when(condition)
        def _():
            self.side_copy(0, u).start()

    def forward(self):
        everything = range(len(self.units))
        for k in range(1, self.length):
            for u in everything:
                condition = self.units[u][3]

                @when(both(condition, self.in_line(k)))
                def _():
                    self.left_arrival(k, u).wait_recv()

                    @pl.when(self.has_left)
                    def _():
                        self.left_copy(k, u).start()

                @when(both(condition, self.by_side(k, u)))
                def _():
                    self.side_copy(k, u).start()

                @when(both(condition, self.in_line(-k)))
                def _():
                    self.right_arrival(k, u).wait_recv()

                    @pl.when(self.has_right)
                    def _():
                        self.right_copy(k, u).start()

                @when(both(condition, self.by_side(-k, u)))
                def _():
                    self.side_copy(-k, u).start()

            for u in everything:
                if self.is_half(u):
                    @when(both(self.units[u][3], self.half_round == k))
                    def _():
                        self.side_arrival(0, u).wait_recv()
                        self.half_copy(u).start()

    def finish(self):
        everything = range(len(self.units))
        for u in everything:
            if not self.is_half(u):
                @when(self.units[u][3])
                def _():
                    self.side_arrival(0, u).wait_recv()

        for k in range(1, self.length):
            for u in everything:
                for distance in (k, -k):
                    @when(both(self.units[u][3], self.by_side(distance, u)))
                    def _():
                        self.side_arrival(distance, u).wait_recv()
                        self.side_copy(distance, u).wait_send()

        for u in everything:
            if self.is_half(u):
                @when(self.units[u][3])
                def _():
                    self.half_arrival(u).wait_recv()
                    self.half_copy(u).wait_send()

        for u in everything:
            condition = self.units[u][3]

            @when(condition)
            def _():
                self.side_copy(0, u).wait_send()

            for k in range(self.length):
                @when(both(condition, self.has_left, self.place + k <= self.length - 1))
                def _():
                    self.left_copy(k, u).wait_send()

                @when(both(condition, self.has_right, self.place - k >= 0))
                def _():
                    self.right_copy(k, u).wait_send()


def is_late():
    return lax.axis_index("tp") % 2 == 1


def plan(rows):
    def cut(share):
        return share * rows // SHARES // 16 * 16

    units = []
    for which, runs in enumerate((GATE_RUNS, UP_RUNS)):
        last = 0
        for end, when, halved in runs:
            if cut(end) > cut(last):
                units.append((which, cut(last), cut(end) - cut(last), when, halved))
            last = end
    return units


def first_units(rows):
    late = is_late()
    return [(which, first, size, late if when else None, halved) for which, first, size, when, halved in plan(rows) if when < 2]


def last_units(rows):
    early = jnp.logical_not(is_late())
    return [(which, first, size, early if when < 2 else None, halved) for which, first, size, when, halved in plan(rows) if when]


def first_kernel(
    count, pieces, head,
    train_gate, slow_gate, train_up, slow_up, gain_ref,
    gate_ref, up_ref, scale_gate_ref, scale_up_ref,
    train, slow, gains, sums, heads,
    head_send, head_recv, load_sem, sum_send, sum_recv, *sems,
):
    rows, columns = train_gate.shape
    piece_rows = rows // pieces
    me = lax.axis_index("zero")
    outs = (gate_ref, up_ref)
    scales = (scale_gate_ref, scale_up_ref)
    relay = Relay(count, rows, head, first_units(rows), outs, outs, sems)

    barrier = pltpu.get_barrier_semaphore()
    for step in range(1, count):
        pl.semaphore_signal(barrier, 1, device_id={"zero": lax.rem(me + step, count)}, device_id_type=MESH)

    loads = []
    for which, (t, s) in enumerate(((train_gate, slow_gate), (train_up, slow_up))):
        for p in range(pieces):
            at = pl.ds(p * piece_rows, piece_rows)
            k = (which * pieces + p) * 2
            loads.append((
                pltpu.make_async_copy(t.at[at], train.at[which, at], load_sem.at[k]),
                pltpu.make_async_copy(s.at[at], slow.at[which, at], load_sem.at[k + 1]),
            ))
    for pair in loads:
        for load in pair:
            load.start()

    gains[...] = jnp.broadcast_to(gain_ref[...], (LANES, rows)).T

    def sum_copy(which, step, source, to):
        k = which * (count - 1) + step - 1
        return pltpu.make_async_remote_copy(
            src_ref=sums.at[which, source], dst_ref=sums.at[which, source],
            send_sem=sum_send.at[k], recv_sem=sum_recv.at[k],
            device_id={"zero": to}, device_id_type=MESH,
        )

    for which in range(2):
        def add(i, total):
            at = pl.ds(pl.multiple_of(i * GROUP, GROUP), GROUP)
            gain = jnp.concatenate([gains[at, :]] * (columns // LANES), axis=1)
            gained = (keep_rate * slow[which, at, :] + (1.0 - keep_rate) * train[which, at, :]) * gain
            slow[which, at, :] = gained
            return total + gained * gained

        total = jnp.zeros((GROUP, columns), jnp.float32)
        for p in range(pieces):
            for load in loads[which * pieces + p]:
                load.wait()
            total = lax.fori_loop(p * piece_rows // GROUP, (p + 1) * piece_rows // GROUP, add, total)
        sums[which, me] = jnp.sum(total, axis=0, keepdims=True)
        if which == 0:
            pl.semaphore_wait(barrier, count - 1)
        for step in range(1, count):
            sum_copy(which, step, me, lax.rem(me + step, count)).start()

    def head_copy(slot, to):
        return pltpu.make_async_remote_copy(
            src_ref=slow.at[0, pl.ds(0, head)], dst_ref=heads.at[slot],
            send_sem=head_send.at[slot], recv_sem=head_recv.at[slot],
            device_id={"zero": to}, device_id_type=MESH,
        )

    @pl.when(relay.has_left)
    def _():
        head_copy(0, relay.to_left).start()

    @pl.when(relay.has_right)
    def _():
        head_copy(1, relay.to_right).start()

    head_copy(2, relay.to_side).start()

    for which in range(2):
        for step in range(1, count):
            source = lax.rem(me + count - step, count)
            sum_copy(which, step, source, source).wait_recv()
        total = sums[which, 0]
        for k in range(1, count):
            total = total + sums[which, k]
        scale = jnp.sqrt(total)
        scales[which][...] = scale
        inverse = 1.0 / scale

        def store(first, size):
            start = pl.multiple_of(me * rows + first, GROUP * 2)
            block = slow[which, pl.ds(first, size), :]
            outs[which][pl.ds(start, size), :] = (block * inverse).astype(jnp.bfloat16)

        mine = [(u, unit[1], unit[2]) for u, unit in enumerate(relay.units) if unit[0] == which]
        stored = 0
        for u, first, size in mine:
            ready = min(first + size + LEAD, rows)
            if ready > stored:
                store(stored, ready - stored)
            relay.send_own(u)
            stored = ready
        if stored < rows:
            store(stored, rows - stored)

        if which == 0:
            def use_head(slot, owner, sender):
                head_copy(slot, sender).wait_recv()
                start = pl.multiple_of(owner * rows, GROUP * 2)
                outs[0][pl.ds(start, head), :] = (heads[slot] * inverse).astype(jnp.bfloat16)

            @pl.when(relay.has_right)
            def _():
                use_head(0, relay.to_right, relay.to_right)

            @pl.when(relay.has_left)
            def _():
                use_head(1, relay.to_left, relay.to_left)

            use_head(2, relay.to_side, relay.to_side)

    relay.forward()
    relay.finish()

    for which in range(2):
        for step in range(1, count):
            sum_copy(which, step, me, lax.rem(me + step, count)).wait_send()

    @pl.when(relay.has_left)
    def _():
        head_copy(0, relay.to_left).wait_send()

    @pl.when(relay.has_right)
    def _():
        head_copy(1, relay.to_right).wait_send()

    head_copy(2, relay.to_side).wait_send()


def last_kernel(count, own_ref, token_ref, up_ref, *sems):
    rows = own_ref.shape[0] // count
    relay = Relay(count, rows, 0, last_units(rows), (None, own_ref), (None, up_ref), sems)
    barrier = pltpu.get_barrier_semaphore()

    def greet(to):
        pl.semaphore_signal(barrier, 1, device_id={"zero": to}, device_id_type=MESH)

    @pl.when(relay.has_left)
    def _():
        greet(relay.to_left)

    @pl.when(relay.has_right)
    def _():
        greet(relay.to_right)

    greet(relay.to_side)
    pl.semaphore_wait(barrier, 1 + relay.has_left.astype(jnp.int32) + relay.has_right.astype(jnp.int32))
    for u in range(len(relay.units)):
        relay.send_own(u)
    relay.forward()
    relay.finish()


def phases(rows):
    found = []
    for phase in range(3):
        units = [unit for unit in plan(rows) if unit[0] == 1 and unit[3] == phase]
        if units:
            found.append((phase, units[0][1], sum(unit[2] for unit in units)))
    return found


def run_copies(copies):
    for condition, copy in copies:
        when(condition)(copy.start)
    for condition, copy in copies:
        when(condition)(copy.wait)


def first_store_kernel(count, parts, gate, up, scale_gate, scale_up, gate_out, up_out, scale_gate_out, scale_up_out, token, sem):
    token[...] = jnp.zeros_like(token)
    me, late = lax.axis_index("zero"), is_late()
    rows = up.shape[0] // count
    copies = []

    def add(condition, held, out):
        copies.append((condition, pltpu.make_async_copy(held, out, sem.at[len(copies)])))

    whole = gate.shape[0] // parts
    for k in range(parts):
        at = pl.ds(k * whole, whole)
        add(None, gate.at[at], gate_out.at[at])
    for owner in range(count):
        for phase, first, size in phases(rows):
            at = pl.ds(owner * rows + first, size)
            condition = (None, jnp.logical_or(late, me == owner), me == owner)[phase]
            add(condition, up.at[at], up_out.at[at])
    add(None, scale_gate.at[0], scale_gate_out)
    add(None, scale_up.at[0], scale_up_out)
    run_copies(copies)


def last_store_kernel(count, up, up_before, up_out, sem):
    me, early = lax.axis_index("zero"), jnp.logical_not(is_late())
    rows = up.shape[0] // count
    copies = []
    for owner in range(count):
        for phase, first, size in phases(rows):
            if phase:
                at = pl.ds(owner * rows + first, size)
                condition = jnp.logical_and(early, me != owner) if phase == 1 else me != owner
                copies.append((condition, pltpu.make_async_copy(up.at[at], up_out.at[at], sem.at[len(copies)])))
    run_copies(copies)


def solution(mesh):
    count = mesh.shape["zero"]

    def body(train_gate, slow_gate, train_up, slow_up, norm_gain):
        rows, columns = train_gate.shape
        pieces = max(1, min(2, rows // 64))
        whens = [unit[3] for unit in plan(rows)]
        length = count // SIDE
        full = (rows * count, columns)
        block = pltpu.VMEM(full, jnp.bfloat16)
        scale = pltpu.VMEM((1, columns), jnp.float32)
        token = pltpu.VMEM((GROUP, LANES), jnp.float32)
        wide = jax.ShapeDtypeStruct(full, jnp.bfloat16)
        vmem, held = pl.BlockSpec(memory_space=pltpu.VMEM), pl.BlockSpec(memory_space=pltpu.HBM)
        dma = lambda n: pltpu.SemaphoreType.DMA((n,))

        def relay_sems(n):
            line, across = length * n, (2 * length - 1) * n
            return [dma(line), dma(line), dma(line), dma(line), dma(across), dma(across), dma(n), dma(n)]

        gate, up, scale_gate, scale_up = pl.pallas_call(
            functools.partial(first_kernel, count, pieces, HEAD),
            out_shape=(block, block, scale, scale),
            in_specs=[held] * 4 + [vmem],
            out_specs=(vmem,) * 4,
            scratch_shapes=[
                pltpu.VMEM((2, rows, columns), jnp.float32),
                pltpu.VMEM((2, rows, columns), jnp.float32),
                pltpu.VMEM((rows, LANES), jnp.float32),
                pltpu.VMEM((2, count, 1, columns), jnp.float32),
                pltpu.VMEM((3, HEAD, columns), jnp.float32),
                dma(3), dma(3), dma(4 * pieces), dma(2 * count - 2), dma(2 * count - 2),
                *relay_sems(sum(when < 2 for when in whens)),
            ],
            compiler_params=pltpu.CompilerParams(
                collective_id=0, has_side_effects=True,
                vmem_limit_bytes=VMEM_BYTES - 3 * full[0] * full[1] * 2 - (1 << 20),
            ),
        )(train_gate, slow_gate, train_up, slow_up, norm_gain[None, :])
        parts = 4
        flat = jax.ShapeDtypeStruct((columns,), jnp.float32)
        gate_out, up_out, scale_gate, scale_up, token = pl.pallas_call(
            functools.partial(first_store_kernel, count, parts),
            out_shape=(wide, wide, flat, flat, token),
            in_specs=[vmem] * 4,
            out_specs=(held,) * 4 + (vmem,),
            scratch_shapes=[dma(parts + 3 * count + 2)],
            compiler_params=pltpu.CompilerParams(vmem_limit_bytes=1 << 20),
        )(gate, up, scale_gate, scale_up)
        rest = pl.pallas_call(
            functools.partial(last_kernel, count),
            out_shape=block,
            in_specs=[vmem, vmem],
            out_specs=vmem,
            scratch_shapes=relay_sems(sum(when > 0 for when in whens)),
            compiler_params=pltpu.CompilerParams(collective_id=1, has_side_effects=True, vmem_limit_bytes=1 << 20),
        )(up, token)
        up_out = pl.pallas_call(
            functools.partial(last_store_kernel, count),
            out_shape=wide,
            in_specs=[vmem, held],
            out_specs=held,
            scratch_shapes=[dma(2 * count)],
            input_output_aliases={1: 0},
            compiler_params=pltpu.CompilerParams(vmem_limit_bytes=1 << 20),
        )(rest, up_out)
        return gate_out, up_out, scale_gate, scale_up

    in_specs = (P("zero", "tp"), P("zero", "tp"), P("zero", "tp"), P("zero", "tp"), P("zero"))
    out_specs = (P(None, "tp"), P(None, "tp"), P("tp"), P("tp"))
    return jax.shard_map(body, mesh=mesh, in_specs=in_specs, out_specs=out_specs, check_vma=False)
```

time: 177 us -> 172 us (0.972)
  Pallas kernels: 175 us -> 171 us
    pallas_call x2 -> x4, Pallas kernels: 175 us -> 171 us  [the longest x1 143 us: body(): pl.pallas_call(functools.partial(first_kernel, count, pieces, HEAD), out_...]
where the time goes in v1:
time: 172 us
  Pallas kernels  171 us (99%)
    pallas_call x1, Pallas kernels, body(): pl.pallas_call(functools.partial(first_kernel, count, pieces, HEAD), out_...  143 us
    pallas_call x1, Pallas kernels, body(): pl.pallas_call(functools.partial(last_kernel, count), out_shape=block, in...  21.2 us
    pallas_call x1, Pallas kernels, body(): pl.pallas_call(functools.partial(first_store_kernel, count, parts), out_s...  5.51 us

profile of v1, /device:TPU:1, one launch (start us, length us, event | category | flops | bytes accessed | tf_op | source)
XLA Modules:
  0.0 171.8 jit_solution(15873926351021364295)
XLA Ops:
  0.6 143.1 %shard_map.84 = (bf16[2048,2048]{1,0:T(8,128)(2,1)S(1)}, bf16[2048,2048]{1,0:T(8,128)(2,1)S(1)}, f32[1,2048]{1,0:T(1,128)S(1)}, f32[1,2048]{1,0:T(1,128)S(1)}) custom-call(f32[256,2048]{1,0:T(8,128)} %train_gate.1, f32[256,2048]{1,0:T(8,128)} %slow_gate.1, f32[256,2048]{1,0:T(8,128)} %train_up.1, f32[256,2048]{1,0:T(8,128)} %slow_up.1, f32[1,256]{1,0:T(1,128)} %bitcast.1), custom_call_target="tpu_custom_call" | custom-call | tf_op jit(solution)/shard_map/pallas_call | solution.py:466
  143.7 5.5 %shard_map.85 = (bf16[2048,2048]{1,0:T(8,128)(2,1)}, bf16[2048,2048]{1,0:T(8,128)(2,1)}, f32[2048]{0:T(1024)}, f32[2048]{0:T(1024)}, f32[8,128]{1,0:T(8,128)S(1)}) custom-call(bf16[2048,2048]{1,0:T(8,128)(2,1)S(1)} %get-tuple-element.13.gate, bf16[2048,2048]{1,0:T(8,128)(2,1)S(1)} %get-tuple-element.14.up.own_ref, ...), custom_call_target="tpu_custom_call" | custom-call | tf_op jit(solution)/shard_map/pallas_call | solution.py:487
  149.2 21.2 %shard_map.86.up = bf16[2048,2048]{1,0:T(8,128)(2,1)S(1)} custom-call(bf16[2048,2048]{1,0:T(8,128)(2,1)S(1)} %get-tuple-element.14.up.own_ref, f32[8,128]{1,0:T(8,128)S(1)} %get-tuple-element.18.token_ref), custom_call_target="tpu_custom_call" | custom-call | tf_op jit(solution)/shard_map/pallas_call | solution.py:495
  170.4 1.4 shard_map.87

commit v2 on v1

--- a/solution.py
+++ b/solution.py
@@ -15,8 +15,8 @@
 HEAD = 16
 LEAD = 16
 SHARES = 16
-GATE_RUNS = ((8, 0, False), (16, 0, True))
-UP_RUNS = ((3, 0, False), (6, 0, True), (12, 1, False), (16, 2, True))
+GATE_RUNS = ((10, 0, False), (16, 0, True))
+UP_RUNS = ((5, 0, True), (12, 1, False), (16, 2, True))
 VMEM_BYTES = 67_043_328
 
 
@@ -44,6 +44,8 @@
         self.is_even = place % 2 == 0
         self.twin = place + 1 - 2 * (place % 2)
         self.to_twin = self.twin * SIDE + side
+        self.is_inner = both(place > 0, place < length - 1)
+        self.twin_is_inner = both(self.twin > 0, self.twin < length - 1)
         self.half_round = jnp.maximum(jnp.where(self.is_even, place, length - 1 - place), 1)
 
     def skipped(self, distance, u):
@@ -101,12 +103,17 @@
     def in_line(self, distance):
         return self.place + distance <= self.length - 1 if distance > 0 else self.place + distance >= 0
 
+    def gets_half(self, u):
+        return None if self.is_half(u) else self.is_inner
+
+    def sends_half(self, u):
+        return None if self.is_half(u) else self.twin_is_inner
+
     def by_side(self, distance, u):
         ok = self.in_line(distance)
-        if self.is_half(u) and distance == 1:
-            ok = jnp.logical_and(ok, jnp.logical_not(self.is_even))
-        if self.is_half(u) and distance == -1:
-            ok = jnp.logical_and(ok, self.is_even)
+        if distance in (1, -1):
+            is_twin = self.is_even if distance == 1 else jnp.logical_not(self.is_even)
+            ok = jnp.logical_and(ok, jnp.logical_not(both(is_twin, self.gets_half(u))))
         return ok
 
     def send_own(self, u):
@@ -155,50 +162,59 @@
                     self.side_copy(-k, u).start()
 
             for u in everything:
-                if self.is_half(u):
-                    @when(both(self.units[u][3], self.half_round == k))
-                    def _():
-                        self.side_arrival(0, u).wait_recv()
-                        self.half_copy(u).start()
+                @when(both(self.units[u][3], self.half_round == k, self.sends_half(u)))
+                def _():
+                    self.side_arrival(0, u).wait_recv()
+                    self.half_copy(u).start()
 
     def finish(self):
         everything = range(len(self.units))
-        for u in everything:
-            if not self.is_half(u):
-                @when(self.units[u][3])
-                def _():
-                    self.side_arrival(0, u).wait_recv()
-
-        for k in range(1, self.length):
+
+        def end_half(u):
+            @when(both(self.units[u][3], self.gets_half(u)))
+            def _():
+                self.half_arrival(u).wait_recv()
+
+            @when(both(self.units[u][3], self.sends_half(u)))
+            def _():
+                self.half_copy(u).wait_send()
+
+        for k in range(self.length):
+            if k == self.length - 1:
+                for u in everything:
+                    if not self.is_half(u):
+                        end_half(u)
+
             for u in everything:
-                for distance in (k, -k):
-                    @when(both(self.units[u][3], self.by_side(distance, u)))
+                condition = self.units[u][3]
+
+                @when(both(condition, self.has_left, self.place + k <= self.length - 1))
+                def _():
+                    self.left_copy(k, u).wait_send()
+
+                @when(both(condition, self.has_right, self.place - k >= 0))
+                def _():
+                    self.right_copy(k, u).wait_send()
+
+                if k == 0:
+                    @when(condition)
                     def _():
-                        self.side_arrival(distance, u).wait_recv()
-                        self.side_copy(distance, u).wait_send()
+                        self.side_copy(0, u).wait_send()
+
+                    if not self.is_half(u):
+                        @when(both(condition, jnp.logical_not(self.twin_is_inner)))
+                        def _():
+                            self.side_arrival(0, u).wait_recv()
+                else:
+                    for distance in (k, -k):
+                        @when(both(condition, self.by_side(distance, u)))
+                        def _():
+                            self.side_arrival(distance, u).wait_recv()
+                            self.side_copy(distance, u).wait_send()
 
         for u in everything:
             if self.is_half(u):
-                @when(self.units[u][3])
-                def _():
-                    self.half_arrival(u).wait_recv()
-                    self.half_copy(u).wait_send()
-
-        for u in everything:
-            condition = self.units[u][3]
-
-            @when(condition)
-            def _():
-                self.side_copy(0, u).wait_send()
-
-            for k in range(self.length):
-                @when(both(condition, self.has_left, self.place + k <= self.length - 1))
-                def _():
-                    self.left_copy(k, u).wait_send()
-
-                @when(both(condition, self.has_right, self.place - k >= 0))
-                def _():
-                    self.right_copy(k, u).wait_send()
+                end_half(u)
 
 
 def is_late():
@@ -270,6 +286,24 @@
             device_id={"zero": to}, device_id_type=MESH,
         )
 
+    def head_copy(slot, to):
+        return pltpu.make_async_remote_copy(
+            src_ref=slow.at[0, pl.ds(0, head)], dst_ref=heads.at[slot],
+            send_sem=head_send.at[slot], recv_sem=head_recv.at[slot],
+            device_id={"zero": to}, device_id_type=MESH,
+        )
+
+    def send_heads():
+        @pl.when(relay.has_left)
+        def _():
+            head_copy(0, relay.to_left).start()
+
+        @pl.when(relay.has_right)
+        def _():
+            head_copy(1, relay.to_right).start()
+
+        head_copy(2, relay.to_side).start()
+
     for which in range(2):
         def add(i, total):
             at = pl.ds(pl.multiple_of(i * GROUP, GROUP), GROUP)
@@ -282,29 +316,14 @@
         for p in range(pieces):
             for load in loads[which * pieces + p]:
                 load.wait()
-            total = lax.fori_loop(p * piece_rows // GROUP, (p + 1) * piece_rows // GROUP, add, total)
+            total = lax.fori_loop(p * piece_rows // GROUP, (p + 1) * piece_rows // GROUP, add, total, unroll=2)
         sums[which, me] = jnp.sum(total, axis=0, keepdims=True)
         if which == 0:
             pl.semaphore_wait(barrier, count - 1)
         for step in range(1, count):
             sum_copy(which, step, me, lax.rem(me + step, count)).start()
-
-    def head_copy(slot, to):
-        return pltpu.make_async_remote_copy(
-            src_ref=slow.at[0, pl.ds(0, head)], dst_ref=heads.at[slot],
-            send_sem=head_send.at[slot], recv_sem=head_recv.at[slot],
-            device_id={"zero": to}, device_id_type=MESH,
-        )
-
-    @pl.when(relay.has_left)
-    def _():
-        head_copy(0, relay.to_left).start()
-
-    @pl.when(relay.has_right)
-    def _():
-        head_copy(1, relay.to_right).start()
-
-    head_copy(2, relay.to_side).start()
+        if which == 0:
+            send_heads()
 
     for which in range(2):
         for step in range(1, count):
@@ -349,9 +368,6 @@
 
             use_head(2, relay.to_side, relay.to_side)
 
-    relay.forward()
-    relay.finish()
-
     for which in range(2):
         for step in range(1, count):
             sum_copy(which, step, me, lax.rem(me + step, count)).wait_send()
@@ -365,6 +381,8 @@
         head_copy(1, relay.to_right).wait_send()
 
     head_copy(2, relay.to_side).wait_send()
+    relay.forward()
+    relay.finish()
 
 
 def last_kernel(count, own_ref, token_ref, up_ref, *sems):
@@ -448,7 +466,7 @@
 
     def body(train_gate, slow_gate, train_up, slow_up, norm_gain):
         rows, columns = train_gate.shape
-        pieces = max(1, min(2, rows // 64))
+        pieces = max(1, min(4, rows // 64))
         whens = [unit[3] for unit in plan(rows)]
         length = count // SIDE
         full = (rows * count, columns)

time: 172 us -> 171 us (level)
    pallas_call x1, Pallas kernels: 143 us -> 140 us  [body(): pl.pallas_call(functools.partial(first_kernel, count, pieces, HEAD), out_...]
    pallas_call x1, Pallas kernels: 21.2 us -> 23.8 us  [body(): pl.pallas_call(functools.partial(last_kernel, count), out_shape=block, in...]
where the time goes in v2:
time: 171 us
  Pallas kernels  170 us (99%)
    pallas_call x1, Pallas kernels, body(): pl.pallas_call(functools.partial(first_kernel, count, pieces, HEAD), out_...  140 us
    pallas_call x1, Pallas kernels, body(): pl.pallas_call(functools.partial(last_kernel, count), out_shape=block, in...  23.8 us
    pallas_call x1, Pallas kernels, body(): pl.pallas_call(functools.partial(first_store_kernel, count, parts), out_s...  5.51 us

profile of v2, /device:TPU:1, one launch (start us, length us, event | category | flops | bytes accessed | tf_op | source)
XLA Modules:
  0.0 171.1 jit_solution(13110452707317025168)
XLA Ops:
  0.6 139.7 %shard_map.84 = (bf16[2048,2048]{1,0:T(8,128)(2,1)S(1)}, bf16[2048,2048]{1,0:T(8,128)(2,1)S(1)}, f32[1,2048]{1,0:T(1,128)S(1)}, f32[1,2048]{1,0:T(1,128)S(1)}) custom-call(f32[256,2048]{1,0:T(8,128)} %train_gate.1, f32[256,2048]{1,0:T(8,128)} %slow_gate.1, f32[256,2048]{1,0:T(8,128)} %train_up.1, f32[256,2048]{1,0:T(8,128)} %slow_up.1, f32[1,256]{1,0:T(1,128)} %bitcast.1), custom_call_target="tpu_custom_call" | custom-call | tf_op jit(solution)/shard_map/pallas_call | solution.py:484
  140.4 5.5 %shard_map.85 = (bf16[2048,2048]{1,0:T(8,128)(2,1)}, bf16[2048,2048]{1,0:T(8,128)(2,1)}, f32[2048]{0:T(1024)}, f32[2048]{0:T(1024)}, f32[8,128]{1,0:T(8,128)S(1)}) custom-call(bf16[2048,2048]{1,0:T(8,128)(2,1)S(1)} %get-tuple-element.13.gate, bf16[2048,2048]{1,0:T(8,128)(2,1)S(1)} %get-tuple-element.14.up.own_ref, ...), custom_call_target="tpu_custom_call" | custom-call | tf_op jit(solution)/shard_map/pallas_call | solution.py:505
  145.9 23.8 %shard_map.86.up = bf16[2048,2048]{1,0:T(8,128)(2,1)S(1)} custom-call(bf16[2048,2048]{1,0:T(8,128)(2,1)S(1)} %get-tuple-element.14.up.own_ref, f32[8,128]{1,0:T(8,128)S(1)} %get-tuple-element.18.token_ref), custom_call_target="tpu_custom_call" | custom-call | tf_op jit(solution)/shard_map/pallas_call | solution.py:513
  169.7 1.4 shard_map.87

commit v3 on v2

--- a/solution.py
+++ b/solution.py
@@ -15,8 +15,8 @@
 HEAD = 16
 LEAD = 16
 SHARES = 16
-GATE_RUNS = ((10, 0, False), (16, 0, True))
-UP_RUNS = ((5, 0, True), (12, 1, False), (16, 2, True))
+GATE_RUNS = ((5, 0, False), (16, 0, True))
+UP_RUNS = ((5, 0, False), (12, 1, False), (16, 2, True))
 VMEM_BYTES = 67_043_328
 
 

time: 171 us -> 171 us (level)
  no operation moved by 1% of the time
where the time goes in v3:
time: 171 us
  Pallas kernels  170 us (99%)
    pallas_call x1, Pallas kernels, body(): pl.pallas_call(functools.partial(first_kernel, count, pieces, HEAD), out_...  138 us
    pallas_call x1, Pallas kernels, body(): pl.pallas_call(functools.partial(last_kernel, count), out_shape=block, in...  25.2 us
    pallas_call x1, Pallas kernels, body(): pl.pallas_call(functools.partial(first_store_kernel, count, parts), out_s...  5.51 us

profile of v3, /device:TPU:1, one launch (start us, length us, event | category | flops | bytes accessed | tf_op | source)
XLA Modules:
  0.0 171.1 jit_solution(17598620398028408549)
XLA Ops:
  0.6 138.4 %shard_map.84 = (bf16[2048,2048]{1,0:T(8,128)(2,1)S(1)}, bf16[2048,2048]{1,0:T(8,128)(2,1)S(1)}, f32[1,2048]{1,0:T(1,128)S(1)}, f32[1,2048]{1,0:T(1,128)S(1)}) custom-call(f32[256,2048]{1,0:T(8,128)} %train_gate.1, f32[256,2048]{1,0:T(8,128)} %slow_gate.1, f32[256,2048]{1,0:T(8,128)} %train_up.1, f32[256,2048]{1,0:T(8,128)} %slow_up.1, f32[1,256]{1,0:T(1,128)} %bitcast.1), custom_call_target="tpu_custom_call" | custom-call | tf_op jit(solution)/shard_map/pallas_call | solution.py:484
  139.0 5.5 %shard_map.85 = (bf16[2048,2048]{1,0:T(8,128)(2,1)}, bf16[2048,2048]{1,0:T(8,128)(2,1)}, f32[2048]{0:T(1024)}, f32[2048]{0:T(1024)}, f32[8,128]{1,0:T(8,128)S(1)}) custom-call(bf16[2048,2048]{1,0:T(8,128)(2,1)S(1)} %get-tuple-element.13.gate, bf16[2048,2048]{1,0:T(8,128)(2,1)S(1)} %get-tuple-element.14.up.own_ref, ...), custom_call_target="tpu_custom_call" | custom-call | tf_op jit(solution)/shard_map/pallas_call | solution.py:505
  144.5 25.2 %shard_map.86.up = bf16[2048,2048]{1,0:T(8,128)(2,1)S(1)} custom-call(bf16[2048,2048]{1,0:T(8,128)(2,1)S(1)} %get-tuple-element.14.up.own_ref, f32[8,128]{1,0:T(8,128)S(1)} %get-tuple-element.18.token_ref), custom_call_target="tpu_custom_call" | custom-call | tf_op jit(solution)/shard_map/pallas_call | solution.py:513
  169.7 1.4 shard_map.87
